TPU v7x, 512 devices: a whole 4x4x16 slice. The times are simulated.
512 devices in a mesh: row: 32 (over x_lo, z), col: 16 (over y, x_hi, core).
Axes of the slice: x: 4 (x_hi: 2, x_lo: 2; x = x_hi * 2 + x_lo), y: 4, z: 16, core: 2. Of those that a mesh axis runs over, the one named last changes fastest.
Arguments:
- gradient: bfloat16 [8192, 28672], P('row', 'col'), may hold values from -6 to 6
- projector: bfloat16 [8192, 1024], P('row'), may hold values from -0.375 to 0.375
- first_moment: float32 [1024, 28672], P('row', 'col'), may hold values from -6 to 6
- second_moment: float32 [1024, 28672], P('row', 'col'), may hold values from 5e-05 to 0.12, as said below
Outputs:
- update: bfloat16 [8192, 28672], P('row', 'col')
- first_new: float32 [1024, 28672], P('row', 'col')
- second_new: float32 [1024, 28672], P('row', 'col')
Inputs may be any that keep to these rules, and one draw needn't show every extreme that they name: `second_moment`: entries are positive.
All inputs are finite; a program needn't handle non-finite values.
Results may differ from a plain program's by a relative error of at most 0.038.
Values may be sent and summed in bfloat16 or wider, within the bound.
No kernel may reach another device: no remote copies, remote signals or barrier semaphores. Data moves between devices by JAX's collectives and lax.ppermute only.
A program may use at most 64 MiB of HBM per device.

v0:
```python
import jax
import jax.numpy as jnp
from jax import lax
from jax.sharding import Mesh
from jax.sharding import PartitionSpec as P

FF = 28672
R = 1024
LANES = 128
ROW = ("x_lo", "z_hi", "z_lo")
COL = ("y", "x_hi", "core")
SQUARE = ("x_lo", "z_lo")
decay_first = 0.9
decay_second = 0.999
bias_first = 1.0 - 0.9**10
bias_second = 1.0 - 0.999**10
epsilon = 1e-08
clip_limit = 0.5


def exchanged(pieces, axes):
    return lax.all_to_all(pieces, axes, split_axis=0, concat_axis=0, tiled=True)


def spread(block, axes):
    return exchanged(jnp.broadcast_to(block, (lax.axis_size(axes), *block.shape)), axes)


def column_blocks(array, parts, width):
    rows, columns = array.shape
    array = jnp.pad(array, ((0, 0), (0, parts * width - columns)))
    return array.reshape(rows, parts, width).swapaxes(0, 1)


def side_by_side(blocks, columns):
    return blocks.swapaxes(0, 1).reshape(blocks.shape[1], -1)[:, :columns]


def summed_everywhere(value):
    value = jnp.full((8, LANES), value, jnp.float32)
    for axes in (SQUARE, "z_hi", COL):
        value = jnp.sum(spread(value, axes), axis=0)
    return value[0, 0]


def local(gradient, projector, first_moment, second_moment):
    block_rows, columns = gradient.shape
    ranks = projector.shape[1]
    rows = first_moment.shape[0]
    square = lax.axis_size(SQUARE)
    z_hi, z_lo = (lax.axis_size("z_hi"), lax.axis_size("z_lo"))
    width = -(-columns // (square * LANES)) * LANES
    half = ranks // 2
    basis = projector.reshape(block_rows, -1, z_hi, z_lo * rows).swapaxes(1, 2)
    basis = basis.reshape(block_rows, ranks)
    own_half = lax.dynamic_slice_in_dim(basis, lax.axis_index("core") * half, half, 1)
    halves = spread(spread(own_half, SQUARE).reshape(square * block_rows, half), "core")
    block = exchanged(column_blocks(gradient, square, width), SQUARE)
    block = block.reshape(square * block_rows, width)
    partial = jnp.concatenate(
        [
            lax.dot_general(
                halves[k], block, (((0,), (0,)), ((), ())), preferred_element_type=jnp.float32
            ).astype(jnp.bfloat16)
            for k in range(2)
        ]
    )
    summed = lax.psum_scatter(
        partial.reshape(z_hi, ranks // z_hi, width), "z_hi", scatter_dimension=0, tiled=True
    )
    lowrank = exchanged(summed.reshape(square, rows, width), SQUARE)
    lowrank = side_by_side(lowrank, columns).astype(jnp.float32)
    first_new = decay_first * first_moment + (1.0 - decay_first) * lowrank
    second_new = decay_second * second_moment + (1.0 - decay_second) * lowrank * lowrank
    direction = first_new / bias_first / (jnp.sqrt(second_new / bias_second) + epsilon)
    step = exchanged(column_blocks(direction.astype(jnp.bfloat16), square, width), SQUARE)
    step = lax.all_gather(step.reshape(square * rows, width), "z_hi", axis=0, tiled=True)
    total = summed_everywhere(jnp.sum(direction * direction))
    root_mean = jnp.sqrt(total / (R * FF) + 1e-06)
    factor = jnp.minimum(1.0, clip_limit / root_mean)
    whole = lax.optimization_barrier(jnp.concatenate([halves[0], halves[1]], axis=1))
    projected = jnp.dot(whole, step, preferred_element_type=jnp.float32)
    updates = (factor * projected).astype(jnp.bfloat16)
    updates = exchanged(updates.reshape(square, block_rows, width), SQUARE)
    return (side_by_side(updates, columns), first_new, second_new)


def solution(mesh):
    torus = Mesh(mesh.devices.reshape(2, 8, 2, 4, 2, 2), (*ROW, *COL))
    in_specs = (P(ROW, COL), P(ROW, None), P(ROW, COL), P(ROW, COL))
    out_specs = (P(ROW, COL), P(ROW, COL), P(ROW, COL))
    return jax.shard_map(local, mesh=torus, in_specs=in_specs, out_specs=out_specs, check_vma=False)
```

profile of v0, /device:TPU:4, one launch (start us, length us, event | category | flops | bytes accessed | tf_op | source)
XLA Modules:
  0.0 203.9 jit_solution(18431546739833409747)
XLA Ops:
  7.2 1.2 copy.37
  8.5 0.0 copy-start.3
  8.5 0.1 copy.39
  8.7 1.0 broadcast_in_dim.12
  9.7 3.8 %all-to-all-start = ((bf16[4,256,512]{2,1,0:T(8,128)(2,1)}), bf16[4,256,512]{2,1,0:T(8,128)(2,1)S(1)}, u32[]{:S(2)}, u32[]{:S(2)}) async-start(bf16[4,256,512]{2,1,0:T(8,128)(2,1)} %broadcast_in_dim.12), calls=%async_computation | async-start | bytes 2097152 | tf_op jit(solution)/shard_map/all_to_all | solution.py:22
  13.5 0.0 copy-done.3
  13.5 0.5 copy.40
  14.1 0.1 pad.8
  14.1 13.1 %all-to-all-done = bf16[4,256,512]{2,1,0:T(8,128)(2,1)S(1)} async-done(((bf16[4,256,512]{2,1,0:T(8,128)(2,1)}), bf16[4,256,512]{2,1,0:T(8,128)(2,1)S(1)}, u32[]{:S(2)}, u32[]{:S(2)}) %all-to-all-start) | async-done | bytes 1048608 | tf_op jit(solution)/shard_map/all_to_all | solution.py:22
  27.3 15.9 %all_to_all.45 = bf16[4,256,512]{1,2,0:T(8,128)(2,1)S(1)} all-to-all(bf16[4,256,512]{1,2,0:T(8,128)(2,1)S(1)} %bitcast.33), channel_id=1, replica_groups=mesh['x_lo'=2,'z_hi'=8,'z_lo'=2,'y'=4,'x_hi'=2,'core'=2] {'x_lo','z_lo'}, dimensions={0} | all-to-all | bytes 2097152 | tf_op jit(solution)/shard_map/all_to_all | solution.py:22
  43.2 1.5 broadcast_in_dim.13
  44.7 3.8 %all-to-all-start.1 = ((bf16[2,1024,512]{2,1,0:T(8,128)(2,1)}), bf16[2,1024,512]{2,1,0:T(8,128)(2,1)S(1)}, u32[]{:S(2)}, u32[]{:S(2)}) async-start(bf16[2,1024,512]{2,1,0:T(8,128)(2,1)} %broadcast_in_dim.13), calls=%async_computation.1 | async-start | bytes 4194304 | tf_op jit(solution)/shard_map/all_to_all | solution.py:22
  48.5 0.0 reduce-scatter.2.cloned.1.call-start
  48.5 1.3 copy.41
  49.9 0.0 copy-start
  49.9 1.5 all-to-all-done.1
  51.3 2.0 convolution_convert_fusion.1
  53.3 0.0 copy-done
  53.3 0.7 convolution_convert_fusion
  54.1 0.0 copy-start.4
  54.1 0.0 copy-start.5
  54.1 1.0 pad_maximum_fusion.1
  55.1 0.0 reduce-scatter.2.cloned.1.call-update
  55.1 0.0 all-gather.2.cloned.1.call-start
  55.2 57.3 %reduce-scatter.2.cloned.1.call-done = bf16[1,128,512]{2,1,0:T(8,128)(2,1)} async-done(((bf16[8,128,512]{2,1,0:T(8,128)(2,1)}), bf16[1,128,512]{2,1,0:T(8,128)(2,1)}) %reduce-scatter.2.cloned.1.call-update) | async-done | bytes 131088 | tf_op jit(solution)/shard_map/reduce_scatter | solution.py:68
  112.5 8.3 %all_to_all.46 = bf16[4,32,512]{2,1,0:T(8,128)(2,1)S(1)} all-to-all(bf16[4,32,512]{2,1,0:T(8,128)(2,1)} %bitcast.45), channel_id=1, replica_groups=mesh['x_lo'=2,'z_hi'=8,'z_lo'=2,'y'=4,'x_hi'=2,'core'=2] {'x_lo','z_lo'}, dimensions={0} | all-to-all | bytes 262144 | tf_op jit(solution)/shard_map/all_to_all | solution.py:22
  120.8 0.0 copy-done.4
  120.8 0.0 copy-done.5
  120.8 0.8 multiply_reduce_fusion
  121.6 0.0 copy-start.2
  121.6 0.0 copy-start.1
  121.6 0.1 fusion.2
  121.7 0.1 reshape.57
  121.8 8.1 %all_to_all.47 = bf16[4,32,512]{2,1,0:T(8,128)(2,1)} all-to-all(bf16[4,32,512]{2,1,0:T(8,128)(2,1)S(1)} %copy.43), channel_id=1, replica_groups=mesh['x_lo'=2,'z_hi'=8,'z_lo'=2,'y'=4,'x_hi'=2,'core'=2] {'x_lo','z_lo'}, dimensions={0} | all-to-all | bytes 262144 | tf_op jit(solution)/shard_map/all_to_all | solution.py:22
  129.9 0.0 all-gather.2.cloned.1.call-update
  129.9 0.6 broadcast_in_dim_broadcast_in_dim.3
  130.6 7.1 %all_to_all.48 = f32[4,8,128]{2,1,0:T(8,128)S(1)} all-to-all(f32[4,8,128]{2,1,0:T(8,128)S(1)} %broadcast_in_dim_broadcast_in_dim.3), channel_id=1, replica_groups=mesh['x_lo'=2,'z_hi'=8,'z_lo'=2,'y'=4,'x_hi'=2,'core'=2] {'x_lo','z_lo'}, dimensions={0} | all-to-all | bytes 32768 | tf_op jit(solution)/shard_map/all_to_all | solution.py:22
  137.6 0.6 broadcast_in_dim.14
  138.3 0.0 copy-done.2
  138.3 7.5 %all-to-all-start.5 = ((f32[8,8,128]{2,1,0:T(8,128)}), f32[8,8,128]{2,1,0:T(8,128)S(1)}, u32[]{:S(2)}, u32[]{:S(2)}) async-start(f32[8,8,128]{2,1,0:T(8,128)} %broadcast_in_dim.14), calls=%async_computation.6 | async-start | bytes 65536 | tf_op jit(solution)/shard_map/all_to_all | solution.py:22
  145.8 1.2 slice_bitcast_fusion.1
  146.9 0.0 copy-done.1
  147.0 11.8 %all-to-all-done.5 = f32[8,8,128]{2,1,0:T(8,128)S(1)} async-done(((f32[8,8,128]{2,1,0:T(8,128)}), f32[8,8,128]{2,1,0:T(8,128)S(1)}, u32[]{:S(2)}, u32[]{:S(2)}) %all-to-all-start.5) | async-done | bytes 32800 | tf_op jit(solution)/shard_map/all_to_all | solution.py:22
  158.8 0.6 broadcast_in_dim.15
  159.4 7.3 %all-to-all-start.6 = ((f32[16,8,128]{2,1,0:T(8,128)}), f32[16,8,128]{2,1,0:T(8,128)S(1)}, u32[]{:S(2)}, u32[]{:S(2)}) async-start(f32[16,8,128]{2,1,0:T(8,128)} %broadcast_in_dim.15), calls=%async_computation.7 | async-start | bytes 131072 | tf_op jit(solution)/shard_map/all_to_all | solution.py:22
  166.7 1.5 pad_maximum_fusion
  168.2 3.4 %all-to-all-done.6 = f32[16,8,128]{2,1,0:T(8,128)S(1)} async-done(((f32[16,8,128]{2,1,0:T(8,128)}), f32[16,8,128]{2,1,0:T(8,128)S(1)}, u32[]{:S(2)}, u32[]{:S(2)}) %all-to-all-start.6) | async-done | bytes 65568 | tf_op jit(solution)/shard_map/all_to_all | solution.py:22
  171.6 0.5 slice.20
  172.8 6.0 %all-gather.2.cloned.1.call-done = bf16[1024,512]{1,0:T(8,128)(2,1)} async-done(((bf16[128,512]{1,0:T(8,128)(2,1)}), bf16[1024,512]{1,0:T(8,128)(2,1)}) %all-gather.2.cloned.1.call-update) | async-done | bytes 1048592 | tf_op jit(solution)/shard_map/all_gather | solution.py:77
  178.8 2.5 %multiply_convert_fusion = bf16[1024,512]{1,0:T(8,128)(2,1)S(1)} fusion(bf16[1024,1024]{1,0:T(8,128)(2,1)S(1)} %pad_maximum_fusion, bf16[1024,512]{1,0:T(8,128)(2,1)} %all-gather.2.cloned.1.call-done, f32[]{:T(128)} %bitcast.12), kind=kOutput, calls=%fused_computation.1 | convolution fusion | flops 1074790400 | bytes 4194308 | tf_op jit(solution)/shard_map/dot_general | solution.py:82
  181.3 14.6 %all_to_all.49 = bf16[4,256,512]{2,1,0:T(8,128)(2,1)S(1)} all-to-all(bf16[4,256,512]{2,1,0:T(8,128)(2,1)S(1)} %bitcast.40), channel_id=1, replica_groups=mesh['x_lo'=2,'z_hi'=8,'z_lo'=2,'y'=4,'x_hi'=2,'core'=2] {'x_lo','z_lo'}, dimensions={0} | all-to-all | bytes 2097152 | tf_op jit(solution)/shard_map/all_to_all | solution.py:22
  195.9 0.1 copy.46
  196.0 1.0 slice.25
  (8 shorter events, 0.1 us)
Async XLA Ops:
  8.5 5.0 %copy-start.3 = (bf16[256,1792]{1,0:T(8,128)(2,1)S(1)}, bf16[256,1792]{1,0:T(8,128)(2,1)}, u32[]{:S(2)}) copy-start(bf16[256,1792]{1,0:T(8,128)(2,1)} %param.4) | copy-start | bytes 2752516
  9.7 17.6 %all-to-all-start = ((bf16[4,256,512]{2,1,0:T(8,128)(2,1)}), bf16[4,256,512]{2,1,0:T(8,128)(2,1)S(1)}, u32[]{:S(2)}, u32[]{:S(2)}) async-start(bf16[4,256,512]{2,1,0:T(8,128)(2,1)} %broadcast_in_dim.12), calls=%async_computation | async-start | bytes 2097152 | tf_op jit(solution)/shard_map/all_to_all | solution.py:22
  44.7 6.6 %all-to-all-start.1 = ((bf16[2,1024,512]{2,1,0:T(8,128)(2,1)}), bf16[2,1024,512]{2,1,0:T(8,128)(2,1)S(1)}, u32[]{:S(2)}, u32[]{:S(2)}) async-start(bf16[2,1024,512]{2,1,0:T(8,128)(2,1)} %broadcast_in_dim.13), calls=%async_computation.1 | async-start | bytes 4194304 | tf_op jit(solution)/shard_map/all_to_all | solution.py:22
  48.5 64.0 %reduce-scatter.2.cloned.1.call-start = ((), (), s32[]{:S(2)}) async-start(), calls=%async_computation.10 | async-start | bytes 1179648 | tf_op jit(solution)/shard_map/reduce_scatter | solution.py:68
  49.9 3.4 %copy-start = (bf16[4,256,512]{2,1,0:T(8,128)(2,1)S(1)}, bf16[4,256,512]{2,1,0:T(8,128)(2,1)}, u32[]{:S(2)}) copy-start(bf16[4,256,512]{2,1,0:T(8,128)(2,1)} %copy.41) | copy-start | bytes 3145732
  54.1 66.7 %copy-start.4 = (f32[32,1792]{1,0:T(8,128)S(1)}, f32[32,1792]{1,0:T(8,128)}, u32[]{:S(2)}) copy-start(f32[32,1792]{1,0:T(8,128)} %param.6) | copy-start | bytes 688132
  54.1 66.7 %copy-start.5 = (f32[32,1792]{1,0:T(8,128)S(1)}, f32[32,1792]{1,0:T(8,128)}, u32[]{:S(2)}) copy-start(f32[32,1792]{1,0:T(8,128)} %param.7) | copy-start | bytes 688132
  55.1 123.6 %all-gather.2.cloned.1.call-start = ((), (), s32[]{:S(2)}) async-start(), calls=%async_computation.11 | async-start | bytes 1179648 | tf_op jit(solution)/shard_map/all_gather | solution.py:77
  121.6 16.7 %copy-start.2 = (f32[32,1792]{1,0:T(8,128)}, f32[32,1792]{1,0:T(8,128)S(1)}, u32[]{:S(2)}) copy-start(f32[32,1792]{1,0:T(8,128)S(1)} %get-tuple-element.5) | copy-start | bytes 688132
  121.6 25.4 %copy-start.1 = (f32[32,1792]{1,0:T(8,128)}, f32[32,1792]{1,0:T(8,128)S(1)}, u32[]{:S(2)}) copy-start(f32[32,1792]{1,0:T(8,128)S(1)} %get-tuple-element.4) | copy-start | bytes 688132
  138.3 20.5 %all-to-all-start.5 = ((f32[8,8,128]{2,1,0:T(8,128)}), f32[8,8,128]{2,1,0:T(8,128)S(1)}, u32[]{:S(2)}, u32[]{:S(2)}) async-start(f32[8,8,128]{2,1,0:T(8,128)} %broadcast_in_dim.14), calls=%async_computation.6 | async-start | bytes 65536 | tf_op jit(solution)/shard_map/all_to_all | solution.py:22
  159.4 12.1 %all-to-all-start.6 = ((f32[16,8,128]{2,1,0:T(8,128)}), f32[16,8,128]{2,1,0:T(8,128)S(1)}, u32[]{:S(2)}, u32[]{:S(2)}) async-start(f32[16,8,128]{2,1,0:T(8,128)} %broadcast_in_dim.15), calls=%async_computation.7 | async-start | bytes 131072 | tf_op jit(solution)/shard_map/all_to_all | solution.py:22
Sparse Core Ops, SparseCore 0:
  55.3 57.1 reduce-scatter.1
  130.0 48.7 all-gather.1
where the time goes:
time: 205 us; the launch traced here: 204 us
  waiting for transfers between devices  93.1 us (45%)
  blocking collectives  54 us (26%)
  starting transfers between devices  22.5 us (11%)
  between operations  14.9 us (7%)
  local copies, waits for them, and re-layouts  10.8 us (5%)
  matrix products  5.16 us (3%)
  other arithmetic  3.44 us (2%)
    reduce_scatter x1, waiting for transfers between devices, local(): lax.psum_scatter(partial.reshape(z_hi, ranks // z_hi, width), 'z_hi', sca...  57.3 us
    all_to_all x5, blocking collectives, exchanged(): return lax.all_to_all(pieces, axes, split_axis=0, concat_axis=0, tiled=True)  54 us
    all_to_all x4, waiting for transfers between devices, exchanged(): return lax.all_to_all(pieces, axes, split_axis=0, concat_axis=0, tiled=True)  29.8 us
    all_to_all x4, starting transfers between devices, exchanged(): return lax.all_to_all(pieces, axes, split_axis=0, concat_axis=0, tiled=True)  22.4 us
    all_gather x1, waiting for transfers between devices, local(): lax.all_gather(step.reshape(square * rows, width), 'z_hi', axis=0, tiled=...  6 us
  transfers between devices with their start and end apart: 6, of which 6 were waited for; matrix products, arithmetic and copies ran while one was open for 3% of the time, Pallas kernels for 0%

commit v1 on v0

--- a/solution.py
+++ b/solution.py
@@ -74,7 +74,12 @@
     second_new = decay_second * second_moment + (1.0 - decay_second) * lowrank * lowrank
     direction = first_new / bias_first / (jnp.sqrt(second_new / bias_second) + epsilon)
     step = exchanged(column_blocks(direction.astype(jnp.bfloat16), square, width), SQUARE)
-    step = lax.all_gather(step.reshape(square * rows, width), "z_hi", axis=0, tiled=True)
+    step = jnp.concatenate(
+        lax.all_to_all(
+            jnp.stack([step.reshape(square * rows, width)] * lax.axis_size("z_hi")), "z_hi", 0, 0
+        ),
+        axis=0,
+    )
     total = summed_everywhere(jnp.sum(direction * direction))
     root_mean = jnp.sqrt(total / (R * FF) + 1e-06)
     factor = jnp.minimum(1.0, clip_limit / root_mean)

time: 205 us -> 256 us (1.25)
  the two profiles are of different devices: /device:TPU:4 before, /device:TPU:64 now
where the time goes in v1:
time: 256 us; the launch traced here: 255 us
  waiting for transfers between devices  130 us (51%)
  blocking collectives  72.8 us (28%)
  starting transfers between devices  20.6 us (8%)
  between operations  14.9 us (6%)
  local copies, waits for them, and re-layouts  10.2 us (4%)
  matrix products  3.92 us (2%)
    all_to_all x6, blocking collectives, exchanged(): return lax.all_to_all(pieces, axes, split_axis=0, concat_axis=0, tiled=True)  72.8 us
    reduce_scatter x1, waiting for transfers between devices, local(): lax.psum_scatter(partial.reshape(z_hi, ranks // z_hi, width), 'z_hi', sca...  57.1 us
    all_to_all x1, waiting for transfers between devices, local(): lax.all_to_all(jnp.stack([step.reshape(square * rows, width)] * lax.axis_...  51.5 us
    all_to_all x3, waiting for transfers between devices, exchanged(): return lax.all_to_all(pieces, axes, split_axis=0, concat_axis=0, tiled=True)  21.9 us
    all_to_all x3, starting transfers between devices, exchanged(): return lax.all_to_all(pieces, axes, split_axis=0, concat_axis=0, tiled=True)  14.5 us
    all_to_all x1, starting transfers between devices, local(): lax.all_to_all(jnp.stack([step.reshape(square * rows, width)] * lax.axis_...  6.08 us
  transfers between devices with their start and end apart: 5, of which 5 were waited for; matrix products, arithmetic and copies ran while one was open for 1% of the time, Pallas kernels for 0%

profile of v1, /device:TPU:64, one launch (start us, length us, event | category | flops | bytes accessed | tf_op | source)
XLA Modules:
  0.0 255.1 jit_solution(2782611862569417278)
XLA Ops:
  7.2 1.2 copy.37
  8.5 0.0 copy-start.3
  8.5 0.1 copy.39
  8.7 1.0 broadcast_in_dim.12
  9.7 4.1 %all-to-all-start = ((bf16[4,256,512]{2,1,0:T(8,128)(2,1)}), bf16[4,256,512]{2,1,0:T(8,128)(2,1)S(1)}, u32[]{:S(2)}, u32[]{:S(2)}) async-start(bf16[4,256,512]{2,1,0:T(8,128)(2,1)} %broadcast_in_dim.12), calls=%async_computation | async-start | bytes 2097152 | tf_op jit(solution)/shard_map/all_to_all | solution.py:22
  13.8 0.0 copy-done.3
  13.8 0.5 copy.40
  14.4 0.1 pad.8
  14.4 13.0 %all-to-all-done = bf16[4,256,512]{2,1,0:T(8,128)(2,1)S(1)} async-done(((bf16[4,256,512]{2,1,0:T(8,128)(2,1)}), bf16[4,256,512]{2,1,0:T(8,128)(2,1)S(1)}, u32[]{:S(2)}, u32[]{:S(2)}) %all-to-all-start) | async-done | bytes 1048608 | tf_op jit(solution)/shard_map/all_to_all | solution.py:22
  27.5 16.1 %all_to_all.50 = bf16[4,256,512]{1,2,0:T(8,128)(2,1)S(1)} all-to-all(bf16[4,256,512]{1,2,0:T(8,128)(2,1)S(1)} %bitcast.34), channel_id=1, replica_groups=mesh['x_lo'=2,'z_hi'=8,'z_lo'=2,'y'=4,'x_hi'=2,'core'=2] {'x_lo','z_lo'}, dimensions={0} | all-to-all | bytes 2097152 | tf_op jit(solution)/shard_map/all_to_all | solution.py:22
  43.5 1.5 broadcast_in_dim.13
  45.0 3.8 %all-to-all-start.1 = ((bf16[2,1024,512]{2,1,0:T(8,128)(2,1)}), bf16[2,1024,512]{2,1,0:T(8,128)(2,1)S(1)}, u32[]{:S(2)}, u32[]{:S(2)}) async-start(bf16[2,1024,512]{2,1,0:T(8,128)(2,1)} %broadcast_in_dim.13), calls=%async_computation.1 | async-start | bytes 4194304 | tf_op jit(solution)/shard_map/all_to_all | solution.py:22
  48.8 0.0 reduce-scatter.2.cloned.1.call-start
  48.8 1.3 copy.41
  50.2 0.0 copy-start
  50.2 1.5 all-to-all-done.1
  51.6 2.0 convolution_convert_fusion.1
  53.6 0.0 copy-done
  53.6 0.7 convolution_convert_fusion
  54.3 0.0 copy-start.4
  54.3 0.0 copy-start.5
  54.4 1.0 pad_maximum_fusion.1
  55.4 0.0 reduce-scatter.2.cloned.1.call-update
  55.4 57.1 %reduce-scatter.2.cloned.1.call-done = bf16[1,128,512]{2,1,0:T(8,128)(2,1)} async-done(((bf16[8,128,512]{2,1,0:T(8,128)(2,1)}), bf16[1,128,512]{2,1,0:T(8,128)(2,1)}) %reduce-scatter.2.cloned.1.call-update) | async-done | bytes 131088 | tf_op jit(solution)/shard_map/reduce_scatter | solution.py:68
  112.5 8.3 %all_to_all.51 = bf16[4,32,512]{2,1,0:T(8,128)(2,1)S(1)} all-to-all(bf16[4,32,512]{2,1,0:T(8,128)(2,1)} %bitcast.47), channel_id=1, replica_groups=mesh['x_lo'=2,'z_hi'=8,'z_lo'=2,'y'=4,'x_hi'=2,'core'=2] {'x_lo','z_lo'}, dimensions={0} | all-to-all | bytes 262144 | tf_op jit(solution)/shard_map/all_to_all | solution.py:22
  120.8 0.0 copy-done.4
  120.8 0.0 copy-done.5
  120.8 0.8 multiply_reduce_fusion
  121.6 0.0 copy-start.2
  121.6 0.0 copy-start.1
  121.6 0.6 broadcast_in_dim_broadcast_in_dim.3
  122.2 7.1 %all_to_all.52 = f32[4,8,128]{2,1,0:T(8,128)S(1)} all-to-all(f32[4,8,128]{2,1,0:T(8,128)S(1)} %broadcast_in_dim_broadcast_in_dim.3), channel_id=1, replica_groups=mesh['x_lo'=2,'z_hi'=8,'z_lo'=2,'y'=4,'x_hi'=2,'core'=2] {'x_lo','z_lo'}, dimensions={0} | all-to-all | bytes 32768 | tf_op jit(solution)/shard_map/all_to_all | solution.py:22
  129.3 17.2 %all_to_all.53 = f32[8,8,128]{2,1,0:T(8,128)S(1)} all-to-all(f32[8,8,128]{2,1,0:T(8,128)S(1)} %broadcast_in_dim.14), channel_id=1, replica_groups=mesh['x_lo'=2,'z_hi'=8,'z_lo'=2,'y'=4,'x_hi'=2,'core'=2] {'z_hi'}, dimensions={0} | all-to-all | bytes 65536 | tf_op jit(solution)/shard_map/all_to_all | solution.py:22
  146.5 0.6 broadcast_in_dim.15
  147.1 6.6 %all-to-all-start.6 = ((f32[16,8,128]{2,1,0:T(8,128)}), f32[16,8,128]{2,1,0:T(8,128)S(1)}, u32[]{:S(2)}, u32[]{:S(2)}) async-start(f32[16,8,128]{2,1,0:T(8,128)} %broadcast_in_dim.15), calls=%async_computation.7 | async-start | bytes 131072 | tf_op jit(solution)/shard_map/all_to_all | solution.py:22
  153.8 0.1 fusion.2
  153.9 0.1 reshape.59
  154.0 7.4 %all-to-all-done.6 = f32[16,8,128]{2,1,0:T(8,128)S(1)} async-done(((f32[16,8,128]{2,1,0:T(8,128)}), f32[16,8,128]{2,1,0:T(8,128)S(1)}, u32[]{:S(2)}, u32[]{:S(2)}) %all-to-all-start.6) | async-done | bytes 65568 | tf_op jit(solution)/shard_map/all_to_all | solution.py:22
  161.5 7.4 %all_to_all.54 = bf16[4,32,512]{2,1,0:T(8,128)(2,1)S(1)} all-to-all(bf16[4,32,512]{2,1,0:T(8,128)(2,1)S(1)} %copy.43), channel_id=1, replica_groups=mesh['x_lo'=2,'z_hi'=8,'z_lo'=2,'y'=4,'x_hi'=2,'core'=2] {'x_lo','z_lo'}, dimensions={0} | all-to-all | bytes 262144 | tf_op jit(solution)/shard_map/all_to_all | solution.py:22
  168.9 1.1 stack.3
  169.9 0.0 copy-done.2
  169.9 0.0 copy-done.1
  169.9 6.1 %all-to-all-start.8 = ((bf16[8,128,512]{2,1,0:T(8,128)(2,1)}), bf16[8,128,512]{2,1,0:T(8,128)(2,1)S(1)}, u32[]{:S(2)}, u32[]{:S(2)}) async-start(bf16[8,128,512]{2,1,0:T(8,128)(2,1)} %stack.3), calls=%async_computation.9 | async-start | bytes 2097152 | tf_op jit(solution)/shard_map/all_to_all | solution.py:78
  176.0 0.1 slice_bitcast_fusion.1
  176.1 0.3 pad_maximum_fusion
  176.4 0.5 slice.20
  177.6 51.5 %all-to-all-done.8 = bf16[8,128,512]{2,1,0:T(8,128)(2,1)S(1)} async-done(((bf16[8,128,512]{2,1,0:T(8,128)(2,1)}), bf16[8,128,512]{2,1,0:T(8,128)(2,1)S(1)}, u32[]{:S(2)}, u32[]{:S(2)}) %all-to-all-start.8) | async-done | bytes 1048608 | tf_op jit(solution)/shard_map/all_to_all | solution.py:78
  229.1 1.2 multiply_convert_fusion
  230.4 16.7 %all_to_all.55 = bf16[4,256,512]{2,1,0:T(8,128)(2,1)S(1)} all-to-all(bf16[4,256,512]{2,1,0:T(8,128)(2,1)S(1)} %bitcast.42), channel_id=1, replica_groups=mesh['x_lo'=2,'z_hi'=8,'z_lo'=2,'y'=4,'x_hi'=2,'core'=2] {'x_lo','z_lo'}, dimensions={0} | all-to-all | bytes 2097152 | tf_op jit(solution)/shard_map/all_to_all | solution.py:22
  247.1 0.1 copy.46
  247.3 1.0 slice.25
  (9 shorter events, 0.2 us)
Async XLA Ops:
  8.5 5.3 %copy-start.3 = (bf16[256,1792]{1,0:T(8,128)(2,1)S(1)}, bf16[256,1792]{1,0:T(8,128)(2,1)}, u32[]{:S(2)}) copy-start(bf16[256,1792]{1,0:T(8,128)(2,1)} %param.4) | copy-start | bytes 2752516
  9.7 17.7 %all-to-all-start = ((bf16[4,256,512]{2,1,0:T(8,128)(2,1)}), bf16[4,256,512]{2,1,0:T(8,128)(2,1)S(1)}, u32[]{:S(2)}, u32[]{:S(2)}) async-start(bf16[4,256,512]{2,1,0:T(8,128)(2,1)} %broadcast_in_dim.12), calls=%async_computation | async-start | bytes 2097152 | tf_op jit(solution)/shard_map/all_to_all | solution.py:22
  45.0 6.6 %all-to-all-start.1 = ((bf16[2,1024,512]{2,1,0:T(8,128)(2,1)}), bf16[2,1024,512]{2,1,0:T(8,128)(2,1)S(1)}, u32[]{:S(2)}, u32[]{:S(2)}) async-start(bf16[2,1024,512]{2,1,0:T(8,128)(2,1)} %broadcast_in_dim.13), calls=%async_computation.1 | async-start | bytes 4194304 | tf_op jit(solution)/shard_map/all_to_all | solution.py:22
  48.8 63.7 %reduce-scatter.2.cloned.1.call-start = ((), (), s32[]{:S(2)}) async-start(), calls=%async_computation.11 | async-start | bytes 1179648 | tf_op jit(solution)/shard_map/reduce_scatter | solution.py:68
  50.2 3.4 %copy-start = (bf16[4,256,512]{2,1,0:T(8,128)(2,1)S(1)}, bf16[4,256,512]{2,1,0:T(8,128)(2,1)}, u32[]{:S(2)}) copy-start(bf16[4,256,512]{2,1,0:T(8,128)(2,1)} %copy.41) | copy-start | bytes 3145732
  54.3 66.5 %copy-start.4 = (f32[32,1792]{1,0:T(8,128)S(1)}, f32[32,1792]{1,0:T(8,128)}, u32[]{:S(2)}) copy-start(f32[32,1792]{1,0:T(8,128)} %param.6) | copy-start | bytes 688132
  54.3 66.5 %copy-start.5 = (f32[32,1792]{1,0:T(8,128)S(1)}, f32[32,1792]{1,0:T(8,128)}, u32[]{:S(2)}) copy-start(f32[32,1792]{1,0:T(8,128)} %param.7) | copy-start | bytes 688132
  121.6 48.3 %copy-start.2 = (f32[32,1792]{1,0:T(8,128)}, f32[32,1792]{1,0:T(8,128)S(1)}, u32[]{:S(2)}) copy-start(f32[32,1792]{1,0:T(8,128)S(1)} %get-tuple-element.5) | copy-start | bytes 688132
  121.6 48.3 %copy-start.1 = (f32[32,1792]{1,0:T(8,128)}, f32[32,1792]{1,0:T(8,128)S(1)}, u32[]{:S(2)}) copy-start(f32[32,1792]{1,0:T(8,128)S(1)} %get-tuple-element.4) | copy-start | bytes 688132
  147.1 14.3 %all-to-all-start.6 = ((f32[16,8,128]{2,1,0:T(8,128)}), f32[16,8,128]{2,1,0:T(8,128)S(1)}, u32[]{:S(2)}, u32[]{:S(2)}) async-start(f32[16,8,128]{2,1,0:T(8,128)} %broadcast_in_dim.15), calls=%async_computation.7 | async-start | bytes 131072 | tf_op jit(solution)/shard_map/all_to_all | solution.py:22
  169.9 59.2 %all-to-all-start.8 = ((bf16[8,128,512]{2,1,0:T(8,128)(2,1)}), bf16[8,128,512]{2,1,0:T(8,128)(2,1)S(1)}, u32[]{:S(2)}, u32[]{:S(2)}) async-start(bf16[8,128,512]{2,1,0:T(8,128)(2,1)} %stack.3), calls=%async_computation.9 | async-start | bytes 2097152 | tf_op jit(solution)/shard_map/all_to_all | solution.py:78
Sparse Core Ops, SparseCore 0:
  55.5 56.8 reduce-scatter.1
